TPU v7x, 32 devices: a whole 2x2x4 slice. The times are simulated.
32 devices in a mesh: dp: 8 (over z, core), seq: 4 (over y, x).
Axes of the slice: x: 2, y: 2, z: 4, core: 2. Of those that a mesh axis runs over, the one named last changes fastest.
Arguments:
- tokens: bfloat16 [2, 8, 512, 768], P(None, 'dp', 'seq'), may hold values from -6 to 6
- piece_starts: int32 [2, 8, 2], P(None, 'dp'), may hold values from 0 to 256, as said below
- qkv_weight: bfloat16 [768, 2304], P(('dp', 'seq')), may hold values from -0.21875 to 0.21875
- qv_bias: bfloat16 [1536], P(('dp', 'seq')), may hold values from -1.796875 to 1.796875
- out_weight: bfloat16 [768, 768], P(('dp', 'seq')), may hold values from -1.25 to 1.25
- out_bias: bfloat16 [768], P(('dp', 'seq')), may hold values from -1.796875 to 1.796875
- norm1_gain: bfloat16 [768], P(('dp', 'seq')), may hold values from 0.5 to 1.5
- norm1_bias: bfloat16 [768], P(('dp', 'seq')), may hold values from -1.796875 to 1.796875
- up_weight: bfloat16 [768, 3072], P(('dp', 'seq')), may hold values from -0.21875 to 0.21875
- up_bias: bfloat16 [3072], P(('dp', 'seq')), may hold values from -1.796875 to 1.796875
- down_weight: bfloat16 [3072, 768], P(('dp', 'seq')), may hold values from -0.109375 to 0.109375
- down_bias: bfloat16 [768], P(('dp', 'seq')), may hold values from -1.796875 to 1.796875
- norm2_gain: bfloat16 [768], P(('dp', 'seq')), may hold values from 0.5 to 1.5
- norm2_bias: bfloat16 [768], P(('dp', 'seq')), may hold values from -1.796875 to 1.796875
- grad_out: bfloat16 [2, 8, 512, 768], P(None, 'dp', 'seq'), may hold values from -6 to 6
Outputs:
- layer_out: bfloat16 [2, 8, 512, 768], P(None, 'dp', 'seq')
- tokens_grad: float32 [2, 8, 512, 768], P(None, 'dp', 'seq')
- qkv_weight_grad: float32 [768, 2304], P(('dp', 'seq'))
- qv_bias_grad: float32 [1536], P(('dp', 'seq'))
- out_weight_grad: float32 [768, 768], P(('dp', 'seq'))
- out_bias_grad: float32 [768], P(('dp', 'seq'))
- norm1_gain_grad: float32 [768], P(('dp', 'seq'))
- norm1_bias_grad: float32 [768], P(('dp', 'seq'))
- up_weight_grad: float32 [768, 3072], P(('dp', 'seq'))
- up_bias_grad: float32 [3072], P(('dp', 'seq'))
- down_weight_grad: float32 [3072, 768], P(('dp', 'seq'))
- down_bias_grad: float32 [768], P(('dp', 'seq'))
- norm2_gain_grad: float32 [768], P(('dp', 'seq'))
- norm2_bias_grad: float32 [768], P(('dp', 'seq'))
Inputs may be any that keep to these rules, and one draw needn't show every extreme that they name: `piece_starts`: each sequence's 2 pieces of 256 positions lie inside it, in rising order, without intersection.
All inputs are finite; a program needn't handle non-finite values.
Results may differ from a plain program's by a relative error of at most 0.018.
Values may be sent and summed in bfloat16 or wider, within the bound.
A program may use at most 192 MiB of HBM per device.

v0:
```python
import math
import jax
import jax.numpy as jnp
from jax import lax
from jax.sharding import PartitionSpec as P

HEADS = 12
PIC = 256
NEG = -1e30
EPS = 1e-05


def owners(positions, starts):
    inside = (positions[:, None] >= starts[None, :]) & (positions[:, None] < starts[None, :] + PIC)
    return jnp.max(jnp.where(inside, starts[None, :], -1), axis=1)


def visible_mask(query_pos, query_owner, key_pos, key_owner):
    later = key_pos[None, :] <= query_pos[:, None]
    shared = (key_owner[None, :] == query_owner[:, None]) & (query_owner[:, None] >= 0)
    return later | shared


def normalize(values):
    centre = values - jnp.mean(values, axis=-1, keepdims=True)
    inverse = lax.rsqrt(jnp.mean(centre * centre, axis=-1, keepdims=True) + EPS)
    return (centre * inverse, inverse)


def norm_back(upstream, normed, inverse, gain):
    scaled = upstream * gain
    return inverse * (
        scaled
        - jnp.mean(scaled, axis=-1, keepdims=True)
        - normed * jnp.mean(scaled * normed, axis=-1, keepdims=True)
    )


def matmul(left, right):
    return jnp.dot(left, right, preferred_element_type=jnp.float32)


def left_trans(left, right):
    return lax.dot_general(
        left, right, (((0,), (0,)), ((), ())), preferred_element_type=jnp.float32
    )


def right_trans(left, right):
    return lax.dot_general(
        left, right, (((1,), (1,)), ((), ())), preferred_element_type=jnp.float32
    )


def key_blocks(count):
    size = math.gcd(count, 1024)
    return (size, count // size)


def gather_forward(shards):
    return (
        lax.all_gather(shards[0], ("dp", "seq"), axis=0, tiled=True),
        lax.all_gather(shards[1], ("dp", "seq"), axis=0, tiled=True),
        lax.all_gather(shards[2], ("dp", "seq"), axis=0, tiled=True),
        lax.all_gather(shards[3], ("dp", "seq"), axis=0, tiled=True),
        lax.all_gather(shards[4], ("dp", "seq"), axis=0, tiled=True),
        lax.all_gather(shards[5], ("dp", "seq"), axis=0, tiled=True),
        lax.all_gather(shards[6], ("dp", "seq"), axis=0, tiled=True),
        lax.all_gather(shards[7], ("dp", "seq"), axis=0, tiled=True),
        lax.all_gather(shards[8], ("dp", "seq"), axis=0, tiled=True),
        lax.all_gather(shards[9], ("dp", "seq"), axis=0, tiled=True),
        lax.all_gather(shards[10], ("dp", "seq"), axis=0, tiled=True),
        lax.all_gather(shards[11], ("dp", "seq"), axis=0, tiled=True),
    )


def gather_backward(shards):
    return (
        lax.all_gather(shards[0], ("dp", "seq"), axis=0, tiled=True),
        lax.all_gather(shards[1], ("dp", "seq"), axis=0, tiled=True),
        lax.all_gather(shards[2], ("dp", "seq"), axis=0, tiled=True),
        lax.all_gather(shards[3], ("dp", "seq"), axis=0, tiled=True),
        lax.all_gather(shards[4], ("dp", "seq"), axis=0, tiled=True),
        lax.all_gather(shards[5], ("dp", "seq"), axis=0, tiled=True),
        lax.all_gather(shards[6], ("dp", "seq"), axis=0, tiled=True),
        lax.all_gather(shards[7], ("dp", "seq"), axis=0, tiled=True),
        lax.all_gather(shards[8], ("dp", "seq"), axis=0, tiled=True),
        lax.all_gather(shards[9], ("dp", "seq"), axis=0, tiled=True),
        lax.all_gather(shards[10], ("dp", "seq"), axis=0, tiled=True),
        lax.all_gather(shards[11], ("dp", "seq"), axis=0, tiled=True),
    )


def column_sum(values):
    return jnp.sum(values.astype(jnp.float32), axis=0)


def on_device(
    tokens,
    piece_starts,
    qkv_weight,
    qv_bias,
    out_weight,
    out_bias,
    norm1_gain,
    norm1_bias,
    up_weight,
    up_bias,
    down_weight,
    down_bias,
    norm2_gain,
    norm2_bias,
    grad_out,
):
    shards = (
        qkv_weight,
        qv_bias,
        out_weight,
        out_bias,
        norm1_gain,
        norm1_bias,
        up_weight,
        up_bias,
        down_weight,
        down_bias,
        norm2_gain,
        norm2_bias,
    )
    micro_count = tokens.shape[0]
    rows = tokens.shape[2]
    width = tokens.shape[3]
    head_size = width // HEADS
    scale = 1.0 / math.sqrt(head_size)
    length = rows * lax.axis_size("seq")
    query_pos = lax.axis_index("seq") * rows + jnp.arange(rows, dtype=jnp.int32)
    totals = None
    outputs = []
    input_grads = []
    for micro in range(micro_count):
        params = gather_forward(shards)
        (
            full_qkv,
            full_qvb,
            full_out,
            full_outb,
            full_g1,
            full_b1,
            full_up,
            full_upb,
            full_down,
            full_downb,
            full_g2,
            full_b2,
        ) = params
        starts = piece_starts[micro, 0]
        query_owner = owners(query_pos, starts)
        source = tokens[micro, 0]
        joined = matmul(source, full_qkv)
        queries = (joined[:, :width] + full_qvb[:width].astype(jnp.float32)).astype(jnp.bfloat16)
        keys = joined[:, width : 2 * width].astype(jnp.bfloat16)
        values = (joined[:, 2 * width :] + full_qvb[width:].astype(jnp.float32)).astype(
            jnp.bfloat16
        )
        query_heads = queries.reshape(rows, HEADS, head_size)

        def block_scores(key_block, key_pos):
            scores = (
                jnp.einsum(
                    "qhd,khd->hqk", query_heads, key_block, preferred_element_type=jnp.float32
                )
                * scale
            )
            allowed = visible_mask(query_pos, query_owner, key_pos, owners(key_pos, starts))
            return jnp.where(allowed[None], scores, NEG)

        initial = (
            jnp.full((HEADS, rows), NEG, jnp.float32),
            jnp.zeros((HEADS, rows), jnp.float32),
            jnp.zeros((HEADS, rows, head_size), jnp.float32),
        )
        key_piece = lax.all_gather(keys, "seq", axis=0, tiled=True)
        value_piece = lax.all_gather(values, "seq", axis=0, tiled=True)
        size, count = key_blocks(key_piece.shape[0])

        def one(block, carry):
            run_max, total, accum = carry
            key_block = lax.dynamic_slice_in_dim(key_piece, block * size, size, 0).reshape(
                size, HEADS, head_size
            )
            value_block = lax.dynamic_slice_in_dim(value_piece, block * size, size, 0).reshape(
                size, HEADS, head_size
            )
            key_pos = block * size + jnp.arange(size, dtype=jnp.int32)
            scores = block_scores(key_block, key_pos)
            new_max = jnp.maximum(run_max, jnp.max(scores, axis=-1))
            factor = jnp.exp(run_max - new_max)
            weights = jnp.exp(scores - new_max[:, :, None])
            total = total * factor + jnp.sum(weights, axis=-1)
            accum = accum * factor[:, :, None] + jnp.einsum(
                "hqk,khd->hqd",
                weights.astype(jnp.bfloat16),
                value_block,
                preferred_element_type=jnp.float32,
            )
            return (new_max, total, accum)

        run_max, total, accum = lax.fori_loop(0, count, one, initial)
        lse = run_max + jnp.log(total)
        exact = (accum / total[:, :, None]).transpose(1, 0, 2)
        attended = exact.reshape(rows, width).astype(jnp.bfloat16)
        resid1 = (
            source.astype(jnp.float32) + matmul(attended, full_out) + full_outb.astype(jnp.float32)
        )
        normed1, inverse1 = normalize(resid1)
        gain1 = full_g1.astype(jnp.float32)
        mixed1 = normed1 * gain1 + full_b1.astype(jnp.float32)
        inner = mixed1.astype(jnp.bfloat16)
        pre = matmul(inner, full_up) + full_upb.astype(jnp.float32)
        act = jax.nn.gelu(pre, approximate=False).astype(jnp.bfloat16)
        resid2 = mixed1 + matmul(act, full_down) + full_downb.astype(jnp.float32)
        normed2, inverse2 = normalize(resid2)
        gain2 = full_g2.astype(jnp.float32)
        outputs.append((normed2 * gain2 + full_b2.astype(jnp.float32)).astype(jnp.bfloat16))
        back = gather_backward(shards)
        back_qkv = back[0]
        back_out = back[2]
        back_up = back[6]
        back_down = back[8]
        cotan = grad_out[micro, 0].astype(jnp.float32)
        d_resid2 = norm_back(cotan, normed2, inverse2, gain2)
        grad_g2 = jnp.sum(cotan * normed2, axis=0)
        grad_b2 = jnp.sum(cotan, axis=0)
        d_branch2 = d_resid2.astype(jnp.bfloat16)
        grad_downb = column_sum(d_branch2)
        grad_down = left_trans(act, d_branch2)
        d_act = right_trans(d_branch2, back_down)
        gelu_value, gelu_back = jax.vjp(lambda value: jax.nn.gelu(value, approximate=False), pre)
        d_pre = gelu_back(d_act)[0].astype(jnp.bfloat16)
        grad_upb = column_sum(d_pre)
        grad_up = left_trans(inner, d_pre)
        d_mixed1 = d_resid2 + right_trans(d_pre, back_up)
        d_resid1 = norm_back(d_mixed1, normed1, inverse1, gain1)
        grad_g1 = jnp.sum(d_mixed1 * normed1, axis=0)
        grad_b1 = jnp.sum(d_mixed1, axis=0)
        d_branch1 = d_resid1.astype(jnp.bfloat16)
        grad_outb = column_sum(d_branch1)
        grad_out_w = left_trans(attended, d_branch1)
        d_attended = right_trans(d_branch1, back_out).astype(jnp.bfloat16)
        grad_heads = d_attended.reshape(rows, HEADS, head_size)
        delta = jnp.sum(grad_heads.astype(jnp.float32) * exact, axis=-1).T
        initial_back = (
            jnp.zeros((rows, HEADS, head_size), jnp.float32),
            jnp.zeros((length, width), jnp.float32),
            jnp.zeros((length, width), jnp.float32),
        )
        fold_key_piece = lax.all_gather(keys, "seq", axis=0, tiled=True)
        fold_value_piece = lax.all_gather(values, "seq", axis=0, tiled=True)
        fold_size, fold_count = key_blocks(fold_key_piece.shape[0])

        def fold_one(block, carry):
            query_grad, key_grads, value_grads = carry
            offset = block * fold_size
            key_block = lax.dynamic_slice_in_dim(fold_key_piece, offset, fold_size, 0).reshape(
                fold_size, HEADS, head_size
            )
            value_block = lax.dynamic_slice_in_dim(fold_value_piece, offset, fold_size, 0).reshape(
                fold_size, HEADS, head_size
            )
            key_pos = offset + jnp.arange(fold_size, dtype=jnp.int32)
            probs = jnp.exp(block_scores(key_block, key_pos) - lse[:, :, None])
            d_probs = jnp.einsum(
                "qhd,khd->hqk", grad_heads, value_block, preferred_element_type=jnp.float32
            )
            d_scores = (probs * (d_probs - delta[:, :, None])).astype(jnp.bfloat16)
            query_grad = (
                query_grad
                + jnp.einsum(
                    "hqk,khd->qhd", d_scores, key_block, preferred_element_type=jnp.float32
                )
                * scale
            )
            key_part = (
                jnp.einsum(
                    "hqk,qhd->khd", d_scores, query_heads, preferred_element_type=jnp.float32
                ).reshape(fold_size, width)
                * scale
            )
            value_part = jnp.einsum(
                "hqk,qhd->khd",
                probs.astype(jnp.bfloat16),
                grad_heads,
                preferred_element_type=jnp.float32,
            ).reshape(fold_size, width)
            key_grads = lax.dynamic_update_slice_in_dim(
                key_grads,
                lax.dynamic_slice_in_dim(key_grads, offset, fold_size, 0) + key_part,
                offset,
                0,
            )
            value_grads = lax.dynamic_update_slice_in_dim(
                value_grads,
                lax.dynamic_slice_in_dim(value_grads, offset, fold_size, 0) + value_part,
                offset,
                0,
            )
            return (query_grad, key_grads, value_grads)

        query_grad, key_grads, value_grads = lax.fori_loop(0, fold_count, fold_one, initial_back)
        key_grad, value_grad = (
            lax.psum_scatter(
                key_grads.astype(jnp.bfloat16), "seq", scatter_dimension=0, tiled=True
            ).astype(jnp.float32),
            lax.psum_scatter(
                value_grads.astype(jnp.bfloat16), "seq", scatter_dimension=0, tiled=True
            ).astype(jnp.float32),
        )
        query_share = query_grad.reshape(rows, width)
        d_queries = query_share.astype(jnp.bfloat16)
        d_keys = key_grad.astype(jnp.bfloat16)
        d_values = value_grad.astype(jnp.bfloat16)
        d_joined = jnp.concatenate([d_queries, d_keys, d_values], axis=1)
        grad_qvb = jnp.concatenate([column_sum(d_queries), column_sum(d_values)], axis=0)
        grad_qkv = left_trans(source, d_joined)
        input_grads.append(d_resid1 + right_trans(d_joined, back_qkv))
        terms = (
            grad_qkv,
            grad_qvb,
            grad_out_w,
            grad_outb,
            grad_g1,
            grad_b1,
            grad_up,
            grad_upb,
            grad_down,
            grad_downb,
            grad_g2,
            grad_b2,
        )
        if totals is None:
            totals = terms
        else:
            totals = tuple((first + second for first, second in zip(totals, terms)))
    shares = lax.psum_scatter(totals, ("dp", "seq"), scatter_dimension=0, tiled=True)
    layer_out = jnp.stack(outputs)[:, None]
    tokens_grad = jnp.stack(input_grads)[:, None]
    return (
        layer_out,
        tokens_grad,
        shares[0],
        shares[1],
        shares[2],
        shares[3],
        shares[4],
        shares[5],
        shares[6],
        shares[7],
        shares[8],
        shares[9],
        shares[10],
        shares[11],
    )


def solution(mesh):
    return jax.shard_map(
        on_device,
        mesh=mesh,
        in_specs=(
            P(None, "dp", "seq", None),
            P(None, "dp", None),
            P(("dp", "seq"), None),
            P(("dp", "seq")),
            P(("dp", "seq"), None),
            P(("dp", "seq")),
            P(("dp", "seq")),
            P(("dp", "seq")),
            P(("dp", "seq"), None),
            P(("dp", "seq")),
            P(("dp", "seq"), None),
            P(("dp", "seq")),
            P(("dp", "seq")),
            P(("dp", "seq")),
            P(None, "dp", "seq", None),
        ),
        out_specs=(
            P(None, "dp", "seq", None),
            P(None, "dp", "seq", None),
            P(("dp", "seq"), None),
            P(("dp", "seq")),
            P(("dp", "seq"), None),
            P(("dp", "seq")),
            P(("dp", "seq")),
            P(("dp", "seq")),
            P(("dp", "seq"), None),
            P(("dp", "seq")),
            P(("dp", "seq"), None),
            P(("dp", "seq")),
            P(("dp", "seq")),
            P(("dp", "seq")),
        ),
        check_vma=False,
    )
```

profile of v0, /device:TPU:0, one launch (start us, length us, event | category | flops | bytes accessed | tf_op | source)
XLA Modules:
  0.0 927.6 jit_solution(920579388821818816)
XLA Ops:
  16.8 42.6 %all-reduce.17 = (bf16[3072]{0:T(1024)(128)(2,1)S(1)}, bf16[1536]{0:T(1024)(128)(2,1)S(1)}, bf16[768]{0:T(1024)(128)(2,1)S(1)}, bf16[768]{0:T(1024)(128)(2,1)S(1...) all-reduce(bf16[3072]{0:T(1024)(128)(2,1)S(1)} %dynamic-update-slic, ...), channel_id=1, replica_groups=mesh['dp'=8,'seq'=4] {'dp','seq'}, use_global_device_ids=true, to_apply=%add.4 | all-reduce | flops 9216 | bytes 36864
  64.7 8.9 all-gather.5.cloned.1.call-done
  73.6 2.9 fusion.95
  77.7 12.7 %all_gather.34 = bf16[512,768]{1,0:T(8,128)(2,1)S(1)} all-gather(bf16[128,768]{1,0:T(8,128)(2,1)S(1)} %slice.119), channel_id=1, replica_groups=mesh['dp'=8,'seq'=4] {'seq'}, dimensions={0}, use_global_device_ids=true | all-gather | bytes 983040 | tf_op jit(solution)/shard_map/all_gather | solution.py:181
  91.6 10.5 %all_gather.35 = bf16[512,768]{1,0:T(8,128)(2,1)S(1)} all-gather(bf16[128,768]{1,0:T(8,128)(2,1)S(1)} %get-tuple-element.277), channel_id=1, replica_groups=mesh['dp'=8,'seq'=4] {'seq'}, dimensions={0}, use_global_device_ids=true | all-gather | bytes 983040 | tf_op jit(solution)/shard_map/all_gather | solution.py:182
  104.0 12.6 %all_gather.86 = bf16[512,768]{1,0:T(8,128)(2,1)S(1)} all-gather(bf16[128,768]{1,0:T(8,128)(2,1)S(1)} %slice.118), channel_id=1, replica_groups=mesh['dp'=8,'seq'=4] {'seq'}, dimensions={0}, use_global_device_ids=true | all-gather | bytes 983040 | tf_op jit(solution)/shard_map/all_gather | solution.py:181
  117.8 10.7 %all_gather.87 = bf16[512,768]{1,0:T(8,128)(2,1)S(1)} all-gather(bf16[128,768]{1,0:T(8,128)(2,1)S(1)} %get-tuple-element.271), channel_id=1, replica_groups=mesh['dp'=8,'seq'=4] {'seq'}, dimensions={0}, use_global_device_ids=true | all-gather | bytes 983040 | tf_op jit(solution)/shard_map/all_gather | solution.py:182
  143.2 52.6 %all-gather.9.cloned.1.call-done = bf16[768,3072]{1,0:T(8,128)(2,1)} async-done(((bf16[24,3072]{1,0:T(8,128)(2,1)}), bf16[768,3072]{1,0:T(8,128)(2,1)}) %all-gather.9.cloned.1.call-update) | async-done | bytes 4718608 | tf_op jit(solution)/shard_map/all_gather | solution.py:68
  195.8 8.7 multiply_convert_fusion.5
  204.5 55.9 %all-gather.11.cloned.1.call-done = bf16[3072,768]{1,0:T(8,128)(2,1)} async-done(((bf16[96,768]{1,0:T(8,128)(2,1)}), bf16[3072,768]{1,0:T(8,128)(2,1)}) %all-gather.11.cloned.1.call-update) | async-done | bytes 4718608 | tf_op jit(solution)/shard_map/all_gather | solution.py:70
  260.4 3.6 fusion.139
  264.5 5.5 multiply_convert_fusion.4
  278.8 2.5 convert_reduce_fusion
  281.3 3.1 convert_reduce_fusion.7
  289.1 3.6 fusion.33
  296.2 3.1 multiply_convert_fusion
  304.1 2.7 convolution_convert_fusion.1
  308.5 2.6 fusion.30
  323.9 2.5 convert_reduce_fusion.9
  328.9 19.7 %reduce-scatter.29.cloned.1.call-done = bf16[128,768]{1,0:T(8,128)(2,1)} async-done(((bf16[512,768]{1,0:T(8,128)(2,1)}), bf16[128,768]{1,0:T(8,128)(2,1)}) %reduce-scatter.29.cloned.1.call-update) | async-done | bytes 196624
  349.7 28.0 %reduce-scatter.27.cloned.1.call-done = bf16[128,768]{1,0:T(8,128)(2,1)} async-done(((bf16[512,768]{1,0:T(8,128)(2,1)}), bf16[128,768]{1,0:T(8,128)(2,1)}) %reduce-scatter.27.cloned.1.call-update) | async-done | bytes 196624
  378.8 28.0 %reduce-scatter.25.cloned.1.call-done = bf16[128,768]{1,0:T(8,128)(2,1)} async-done(((bf16[512,768]{1,0:T(8,128)(2,1)}), bf16[128,768]{1,0:T(8,128)(2,1)}) %reduce-scatter.25.cloned.1.call-update) | async-done | bytes 196624
  409.0 4.0 add_bitcast_fusion
  413.0 8.0 copy.87
  423.7 5.1 convolution_add_fusion.1
  431.6 5.1 convolution_add_fusion
  451.6 41.7 %all-reduce.16 = (f32[1536]{0:T(1024)}, f32[768]{0:T(1024)}, f32[768]{0:T(1024)}, f32[768]{0:T(1024)}, f32[3072]{0:T(1024)}, /*index=5*/f32[768]{0:T(1024)}, f32[768]{0:T(1024)}, f32[768]{0:T(1024)}) all-reduce(f32[1536]{0:T(1024)} %maximum_add_fusion, f32[768]{0:T(1024)S(1)} %add.424, ...), channel_id=7, replica_groups=mesh['dp'=8,'seq'=4] {'dp','seq'}, use_global_device_ids=true, to_apply=%region_35.36.clone | all-reduce | flops 9216 | bytes 73728
  503.5 2.6 fusion.56
  508.4 4.1 reduce-scatter.19.cloned.1.call-done
  512.5 124.8 %reduce-scatter.33.cloned.1.call-done = f32[24,2304]{1,0:T(8,128)} async-done(((f32[768,2304]{1,0:T(8,128)}), f32[24,2304]{1,0:T(8,128)}) %reduce-scatter.33.cloned.1.call-update) | async-done | bytes 221200
  637.3 141.6 %reduce-scatter.21.cloned.1.call-done = f32[24,3072]{1,0:T(8,128)} async-done(((f32[768,3072]{1,0:T(8,128)}), f32[24,3072]{1,0:T(8,128)}) %reduce-scatter.21.cloned.1.call-update) | async-done | bytes 294928 | tf_op jit(solution)/shard_map/reduce_scatter | solution.py:343
  778.9 141.5 %reduce-scatter.23.cloned.1.call-done = f32[96,768]{1,0:T(8,128)} async-done(((f32[3072,768]{1,0:T(8,128)}), f32[96,768]{1,0:T(8,128)}) %reduce-scatter.23.cloned.1.call-update) | async-done | bytes 294928 | tf_op jit(solution)/shard_map/reduce_scatter | solution.py:343
  (298 shorter events, 110.7 us)
Async XLA Ops:
  7.2 66.4 %all-gather.5.cloned.1.call-start = ((), (), s32[]{:S(2)}) async-start(), calls=%async_computation.8 | async-start | bytes 3649536 | tf_op jit(solution)/shard_map/all_gather | solution.py:62
  7.9 126.4 %all-gather.7.cloned.1.call-start = ((), (), s32[]{:S(2)}) async-start(), calls=%async_computation.9 | async-start | bytes 1216512 | tf_op jit(solution)/shard_map/all_gather | solution.py:64
  8.7 187.2 %all-gather.9.cloned.1.call-start = ((), (), s32[]{:S(2)}) async-start(), calls=%async_computation.10 | async-start | bytes 4866048 | tf_op jit(solution)/shard_map/all_gather | solution.py:68
  9.4 251.0 %all-gather.11.cloned.1.call-start = ((), (), s32[]{:S(2)}) async-start(), calls=%async_computation.11 | async-start | bytes 4866048 | tf_op jit(solution)/shard_map/all_gather | solution.py:70
  10.0 317.8 %reduce-scatter.31.cloned.1.call-start = ((), (), s32[]{:S(2)}) async-start(), calls=%async_computation.18 | async-start | bytes 983040
  64.7 11.9 %copy-start.22 = (bf16[2,1,128,768]{3,2,1,0:T(8,128)(2,1)S(1)}, bf16[2,1,128,768]{3,2,1,0:T(8,128)(2,1)}, u32[]{:S(2)}) copy-start(bf16[2,1,128,768]{3,2,1,0:T(8,128)(2,1)} %param.15) | copy-start | bytes 1179652
  73.6 3.2 copy-start.1
  77.7 52.0 %copy-start.42 = (bf16[128,768]{0,1:T(8,128)(2,1)}, bf16[128,768]{0,1:T(8,128)(2,1)S(1)}, u32[]{:S(2)}) copy-start(bf16[128,768]{0,1:T(8,128)(2,1)S(1)} %copy.68) | copy-start | bytes 589828
  260.4 4.0 copy-start.3
  260.4 9.6 %slice-start = ((s8[4718592]{0:T(1024)(128)(4,1)}), s8[4194304]{0:T(1024)(128)(4,1)S(1)}, s32[]{:S(2)}) async-start(s8[4718592]{0:T(1024)(128)(4,1)} %bitcast.187), calls=%async_computation.20 | async-start | bytes 8388608
  264.4 5.6 slice-start.1
  264.4 5.6 copy-start.11
  264.4 5.6 copy-start.54
  264.4 5.6 copy-start.62
  264.5 5.6 copy-start.66
  274.0 7.3 copy-start.25
  295.1 53.6 %reduce-scatter.29.cloned.1.call-start = ((), (), s32[]{:S(2)}) async-start(), calls=%async_computation.17 | async-start | bytes 983040
  296.2 4.3 copy-start.45
  304.1 73.6 %reduce-scatter.27.cloned.1.call-start = ((), (), s32[]{:S(2)}) async-start(), calls=%async_computation.16 | async-start | bytes 983040
  313.4 93.4 %reduce-scatter.25.cloned.1.call-start = ((), (), s32[]{:S(2)}) async-start(), calls=%async_computation.15 | async-start | bytes 983040
  314.6 3.3 copy-start.43
  319.6 193.0 %reduce-scatter.19.cloned.1.call-start = ((), (), s32[]{:S(2)}) async-start(), calls=%async_computation.12 | async-start | bytes 2433024 | tf_op jit(solution)/shard_map/reduce_scatter | solution.py:343
  322.5 3.9 copy-start.9
  322.5 314.8 %reduce-scatter.33.cloned.1.call-start = ((), (), s32[]{:S(2)}) async-start(), calls=%async_computation.19 | async-start | bytes 7299072
  326.4 81.5 %copy-start.24 = (bf16[2,1,128,768]{3,2,1,0:T(8,128)(2,1)S(1)}, bf16[2,1,128,768]{3,2,1,0:T(8,128)(2,1)}, u32[]{:S(2)}) copy-start(bf16[2,1,128,768]{3,2,1,0:T(8,128)(2,1)} %param.15) | copy-start | bytes 1179652
  327.8 81.2 %copy-start.48 = (bf16[12,64,128]{2,1,0:T(8,128)(2,1)}, bf16[12,64,128]{2,1,0:T(8,128)(2,1)S(1)}, u32[]{:S(2)}) copy-start(bf16[12,64,128]{2,1,0:T(8,128)(2,1)S(1)} %get-tuple-element.316) | copy-start | bytes 589828
  328.9 80.1 %copy-start.30 = (bf16[128,768]{0,1:T(8,128)(2,1)}, bf16[128,768]{0,1:T(8,128)(2,1)S(1)}, u32[]{:S(2)}) copy-start(bf16[128,768]{0,1:T(8,128)(2,1)S(1)} %copy.86) | copy-start | bytes 589828
  349.7 59.3 %copy-start.40 = (bf16[128,768]{0,1:T(8,128)(2,1)}, bf16[128,768]{0,1:T(8,128)(2,1)S(1)}, u32[]{:S(2)}) copy-start(bf16[128,768]{0,1:T(8,128)(2,1)S(1)} %copy.84) | copy-start | bytes 589828
  378.8 30.2 %copy-start.35 = (bf16[128,768]{0,1:T(8,128)(2,1)}, bf16[128,768]{0,1:T(8,128)(2,1)S(1)}, u32[]{:S(2)}) copy-start(bf16[128,768]{0,1:T(8,128)(2,1)S(1)} %copy.82) | copy-start | bytes 589828
  421.1 357.8 %reduce-scatter.21.cloned.1.call-start = ((), (), s32[]{:S(2)}) async-start(), calls=%async_computation.13 | async-start | bytes 9732096 | tf_op jit(solution)/shard_map/reduce_scatter | solution.py:343
  428.9 491.4 %reduce-scatter.23.cloned.1.call-start = ((), (), s32[]{:S(2)}) async-start(), calls=%async_computation.14 | async-start | bytes 9732096 | tf_op jit(solution)/shard_map/reduce_scatter | solution.py:343
  436.7 66.8 %copy-start.2 = (bf16[768,2304]{1,0:T(8,128)(2,1)S(1)}, bf16[768,2304]{1,0:T(8,128)(2,1)}, u32[]{:S(2)}) copy-start(bf16[768,2304]{1,0:T(8,128)(2,1)} %all-gather.5.cloned.1.call-done) | copy-start | bytes 10616836
  (52 other events, 93.3 us)
Sparse Core Ops, SparseCore 0:
  10.9 62.6 all-gather.4
  76.5 53.7 all-gather.6
  133.1 62.6 all-gather.8
  198.6 61.8 all-gather.10
  295.2 24.4 reduce-scatter.30
  322.4 26.1 reduce-scatter.28
  351.5 26.1 reduce-scatter.26
  380.6 26.1 reduce-scatter.24
  412.7 99.7 reduce-scatter.18
  518.6 118.6 reduce-scatter.32
  643.8 135.0 reduce-scatter.20
  785.2 135.1 reduce-scatter.22
where the time goes:
time: 934 us; the launch traced here: 928 us
  waiting for transfers between devices  608 us (65%)
  blocking collectives  131 us (14%)
  matrix products  86 us (9%)
  local copies, waits for them, and re-layouts  57.4 us (6%)
  other arithmetic  29.5 us (3%)
  between operations  15.5 us (2%)
    reduce_scatter x3, waiting for transfers between devices, on_device(): lax.psum_scatter(totals, ('dp', 'seq'), scatter_dimension=0, tiled=True)  287 us
    unnamed x17, waiting for transfers between devices  203 us
    unnamed x2, blocking collectives  84.3 us
    all_gather x1, waiting for transfers between devices, gather_forward(): lax.all_gather(shards[8], ('dp', 'seq'), axis=0, tiled=True)  55.9 us
    all_gather x1, waiting for transfers between devices, gather_forward(): lax.all_gather(shards[6], ('dp', 'seq'), axis=0, tiled=True)  52.6 us
    unnamed x177, local copies, waits for them, and re-layouts  46.3 us
    all_gather x2, blocking collectives, on_device(): key_piece = lax.all_gather(keys, 'seq', axis=0, tiled=True)  25.3 us
    dot_general x8, matrix products, matmul(): return jnp.dot(left, right, preferred_element_type=jnp.float32)  24.6 us
  transfers between devices with their start and end apart: 12, of which 10 were waited for; matrix products, arithmetic and copies ran while one was open for 14% of the time, Pallas kernels for 0%

commit v1 on v0

--- a/solution.py
+++ b/solution.py
@@ -178,7 +178,16 @@
             jnp.zeros((HEADS, rows), jnp.float32),
             jnp.zeros((HEADS, rows, head_size), jnp.float32),
         )
-        key_piece = lax.all_gather(keys, "seq", axis=0, tiled=True)
+        ways = lax.axis_size("seq")
+        up = [(d, (d + 1) % ways) for d in range(ways)]
+        down = [(d, (d - 1) % ways) for d in range(ways)]
+        earlier, later_2 = ([keys], [keys])
+        for _ in range(ways // 2):
+            earlier.append(lax.ppermute(earlier[-1], "seq", up))
+        for _ in range((ways - 1) // 2):
+            later_2.append(lax.ppermute(later_2[-1], "seq", down))
+        line = jnp.concatenate([*earlier[::-1], *later_2[1:]], axis=0)
+        key_piece = jnp.roll(line, (lax.axis_index("seq") - ways // 2) * keys.shape[0], axis=0)
         value_piece = lax.all_gather(values, "seq", axis=0, tiled=True)
         size, count = key_blocks(key_piece.shape[0])
 

time: 934 us -> 936 us (level)
  waiting for transfers between devices: 608 us -> 546 us
  matrix products: 86 us -> 103 us
  blocking collectives: 131 us -> 146 us
  local copies, waits for them, and re-layouts: 57.4 us -> 70.5 us
  starting transfers between devices: 0.74 us -> 10.5 us
    all_gather x1, waiting for transfers between devices: 52.6 us -> 19 us  [gather_forward(): lax.all_gather(shards[6], ('dp', 'seq'), axis=0, tiled=True)]
    unnamed x17, waiting for transfers between devices: 203 us -> 176 us
    all_gather x2, blocking collectives: 21.2 us -> 33.6 us  [on_device(): value_piece = lax.all_gather(values, 'seq', axis=0, tiled=True)]
    ppermute x0 -> x6, starting transfers between devices: none -> 9.84 us  [the longest x4 6.23 us: on_device(): earlier.append(lax.ppermute(earlier[-1], 'seq', up))]
    unnamed x177 -> x163, local copies, waits for them, and re-layouts: 46.3 us -> 46.3 us
  transfers between devices with their start and end apart: 12 -> 18, of which waited for: 10 -> 10; matrix products, arithmetic and copies ran while one was open for 14% -> 19% of each run, Pallas kernels for 0% -> 0%
where the time goes in v1:
time: 936 us; the launch traced here: 929 us
  waiting for transfers between devices  546 us (58%)
  blocking collectives  146 us (16%)
  matrix products  103 us (11%)
  local copies, waits for them, and re-layouts  70.5 us (8%)
  other arithmetic  37.7 us (4%)
  between operations  15.2 us (2%)
  starting transfers between devices  10.5 us (1%)
    reduce_scatter x3, waiting for transfers between devices, on_device(): lax.psum_scatter(totals, ('dp', 'seq'), scatter_dimension=0, tiled=True)  285 us
    unnamed x17, waiting for transfers between devices  176 us
    unnamed x2, blocking collectives  84.2 us
    all_gather x1, waiting for transfers between devices, gather_forward(): lax.all_gather(shards[8], ('dp', 'seq'), axis=0, tiled=True)  56 us
    unnamed x163, local copies, waits for them, and re-layouts  46.3 us
    all_gather x2, blocking collectives, on_device(): value_piece = lax.all_gather(values, 'seq', axis=0, tiled=True)  33.6 us
    all_gather x2, blocking collectives, on_device(): fold_key_piece = lax.all_gather(keys, 'seq', axis=0, tiled=True)  27.7 us
    dot_general x8, matrix products, left_trans(): lax.dot_general(left, right, (((0,), (0,)), ((), ())), preferred_element_...  25.7 us
  transfers between devices with their start and end apart: 18, of which 10 were waited for; matrix products, arithmetic and copies ran while one was open for 19% of the time, Pallas kernels for 0%

profile of v1, /device:TPU:0, one launch (start us, length us, event | category | flops | bytes accessed | tf_op | source)
XLA Modules:
  0.0 928.6 jit_solution(2604703481502605660)
XLA Ops:
  18.2 42.5 %all-reduce.17 = (bf16[3072]{0:T(1024)(128)(2,1)S(1)}, bf16[1536]{0:T(1024)(128)(2,1)S(1)}, bf16[768]{0:T(1024)(128)(2,1)S(1)}, bf16[768]{0:T(1024)(128)(2,1)S(1...) all-reduce(bf16[3072]{0:T(1024)(128)(2,1)S(1)} %dynamic-update-slic, ...), channel_id=1, replica_groups=mesh['dp'=8,'seq'=4] {'dp','seq'}, use_global_device_ids=true, to_apply=%add.4 | all-reduce | flops 9216 | bytes 36864
  64.1 9.4 %all-gather.5.cloned.1.call-done = bf16[768,2304]{1,0:T(8,128)(2,1)} async-done(((bf16[24,2304]{1,0:T(8,128)(2,1)}), bf16[768,2304]{1,0:T(8,128)(2,1)}) %all-gather.5.cloned.1.call-update) | async-done | bytes 3538960 | tf_op jit(solution)/shard_map/all_gather | solution.py:62
  73.5 2.9 fusion.123
  85.2 21.7 %all_gather.34 = bf16[512,768]{1,0:T(8,128)(2,1)} all-gather(bf16[128,768]{1,0:T(8,128)(2,1)S(1)} %get-tuple-element.278), channel_id=1, replica_groups=mesh['dp'=8,'seq'=4] {'seq'}, dimensions={0}, use_global_device_ids=true | all-gather | bytes 983040 | tf_op jit(solution)/shard_map/all_gather | solution.py:191
  106.9 11.9 %all_gather.83 = bf16[512,768]{1,0:T(8,128)(2,1)} all-gather(bf16[128,768]{1,0:T(8,128)(2,1)S(1)} %get-tuple-element.272), channel_id=1, replica_groups=mesh['dp'=8,'seq'=4] {'seq'}, dimensions={0}, use_global_device_ids=true | all-gather | bytes 983040 | tf_op jit(solution)/shard_map/all_gather | solution.py:191
  126.9 12.1 %all_gather.85 = bf16[512,768]{1,0:T(8,128)(2,1)} all-gather(bf16[128,768]{1,0:T(8,128)(2,1)} %slice.118), channel_id=1, replica_groups=mesh['dp'=8,'seq'=4] {'seq'}, dimensions={0}, use_global_device_ids=true | all-gather | bytes 983040 | tf_op jit(solution)/shard_map/all_gather | solution.py:265
  143.7 3.5 fusion.179
  150.2 4.0 fusion.86
  156.5 3.8 fusion.79
  177.4 19.0 %all-gather.9.cloned.1.call-done = bf16[768,3072]{1,0:T(8,128)(2,1)} async-done(((bf16[24,3072]{1,0:T(8,128)(2,1)}), bf16[768,3072]{1,0:T(8,128)(2,1)}) %all-gather.9.cloned.1.call-update) | async-done | bytes 4718608 | tf_op jit(solution)/shard_map/all_gather | solution.py:68
  196.4 8.7 multiply_convert_fusion.5
  205.2 56.0 %all-gather.11.cloned.1.call-done = bf16[3072,768]{1,0:T(8,128)(2,1)} async-done(((bf16[96,768]{1,0:T(8,128)(2,1)}), bf16[3072,768]{1,0:T(8,128)(2,1)}) %all-gather.11.cloned.1.call-update) | async-done | bytes 4718608 | tf_op jit(solution)/shard_map/all_gather | solution.py:70
  261.1 3.7 fusion.174
  265.3 5.5 multiply_convert_fusion.4
  282.5 3.1 convert_reduce_fusion.7
  290.2 3.8 fusion.47
  297.5 3.3 multiply_convert_fusion
  305.7 15.6 %all_gather.84 = bf16[512,768]{1,0:T(8,128)(2,1)} all-gather(bf16[128,768]{1,0:T(8,128)(2,1)} %slice.119), channel_id=1, replica_groups=mesh['dp'=8,'seq'=4] {'seq'}, dimensions={0}, use_global_device_ids=true | all-gather | bytes 983040 | tf_op jit(solution)/shard_map/all_gather | solution.py:265
  323.6 3.6 fusion.178
  330.2 3.7 fusion.44
  337.5 3.4 multiply_convert_fusion.1
  349.5 3.1 convert_reduce_fusion.9
  358.1 20.9 %reduce-scatter.27.cloned.1.call-done = bf16[128,768]{1,0:T(8,128)(2,1)} async-done(((bf16[512,768]{1,0:T(8,128)(2,1)}), bf16[128,768]{1,0:T(8,128)(2,1)}) %reduce-scatter.27.cloned.1.call-update) | async-done | bytes 196624
  380.7 27.3 %reduce-scatter.25.cloned.1.call-done = bf16[128,768]{1,0:T(8,128)(2,1)} async-done(((bf16[512,768]{1,0:T(8,128)(2,1)}), bf16[128,768]{1,0:T(8,128)(2,1)}) %reduce-scatter.25.cloned.1.call-update) | async-done | bytes 196624
  412.2 4.0 add_bitcast_fusion
  416.2 8.1 copy.95
  427.3 5.1 convolution_add_fusion.1
  435.4 5.1 convolution_add_fusion
  455.3 41.6 %all-reduce.16 = (f32[1536]{0:T(1024)}, f32[768]{0:T(1024)}, f32[768]{0:T(1024)}, f32[768]{0:T(1024)}, f32[3072]{0:T(1024)}, /*index=5*/f32[768]{0:T(1024)}, f32[768]{0:T(1024)}, f32[768]{0:T(1024)}) all-reduce(f32[1536]{0:T(1024)} %maximum_add_fusion, f32[768]{0:T(1024)S(1)} %add.433, ...), channel_id=7, replica_groups=mesh['dp'=8,'seq'=4] {'dp','seq'}, use_global_device_ids=true, to_apply=%region_35.37.clone | all-reduce | flops 9216 | bytes 73728
  513.8 124.7 %reduce-scatter.33.cloned.1.call-done = f32[24,2304]{1,0:T(8,128)} async-done(((f32[768,2304]{1,0:T(8,128)}), f32[24,2304]{1,0:T(8,128)}) %reduce-scatter.33.cloned.1.call-update) | async-done | bytes 221200
  638.4 141.6 %reduce-scatter.21.cloned.1.call-done = f32[24,3072]{1,0:T(8,128)} async-done(((f32[768,3072]{1,0:T(8,128)}), f32[24,3072]{1,0:T(8,128)}) %reduce-scatter.21.cloned.1.call-update) | async-done | bytes 294928 | tf_op jit(solution)/shard_map/reduce_scatter | solution.py:352
  780.0 141.5 %reduce-scatter.23.cloned.1.call-done = f32[96,768]{1,0:T(8,128)} async-done(((f32[3072,768]{1,0:T(8,128)}), f32[96,768]{1,0:T(8,128)}) %reduce-scatter.23.cloned.1.call-update) | async-done | bytes 294928 | tf_op jit(solution)/shard_map/reduce_scatter | solution.py:352
  (302 shorter events, 148.9 us)
Async XLA Ops:
  7.2 66.4 %all-gather.5.cloned.1.call-start = ((), (), s32[]{:S(2)}) async-start(), calls=%async_computation.8 | async-start | bytes 3649536 | tf_op jit(solution)/shard_map/all_gather | solution.py:62
  7.9 160.1 %all-gather.7.cloned.1.call-start = ((), (), s32[]{:S(2)}) async-start(), calls=%async_computation.9 | async-start | bytes 1216512 | tf_op jit(solution)/shard_map/all_gather | solution.py:64
  8.7 187.8 %all-gather.9.cloned.1.call-start = ((), (), s32[]{:S(2)}) async-start(), calls=%async_computation.10 | async-start | bytes 4866048 | tf_op jit(solution)/shard_map/all_gather | solution.py:68
  9.4 251.7 %all-gather.11.cloned.1.call-start = ((), (), s32[]{:S(2)}) async-start(), calls=%async_computation.11 | async-start | bytes 4866048 | tf_op jit(solution)/shard_map/all_gather | solution.py:70
  10.0 344.6 %reduce-scatter.31.cloned.1.call-start = ((), (), s32[]{:S(2)}) async-start(), calls=%async_computation.18 | async-start | bytes 983040
  73.5 6.5 copy-start
  73.5 6.5 copy-start.18
  77.1 7.2 copy-start.50
  77.1 7.2 copy-start.51
  77.1 64.2 %collective-permute-start = (bf16[128,768]{1,0:T(8,128)(2,1)}, bf16[128,768]{1,0:T(8,128)(2,1)}, u32[]{:S(2)}, u32[]{:S(2)}) collective-permute-start(bf16[128,768]{1,0:T(8,128)(2,1)} %slice.119), channel_id=1, source_target_pairs={{0,1},{1,2},{2,3},{3,0},{4,5},{5,6},{6,7},{7,4},{8,9},{9,10},{10,1... | collective-permute-start | bytes 589832 | tf_op jit(solution)/shard_map/ppermute | solution.py:186
  78.7 70.1 %collective-permute-start.2 = (bf16[128,768]{1,0:T(8,128)(2,1)}, bf16[128,768]{1,0:T(8,128)(2,1)}, u32[]{:S(2)}, u32[]{:S(2)}) collective-permute-start(bf16[128,768]{1,0:T(8,128)(2,1)} %slice.119), channel_id=1, source_target_pairs={{0,3},{1,0},{2,1},{3,2},{4,7},{5,4},{6,5},{7,6},{8,11},{9,8},{10,9... | collective-permute-start | bytes 589832 | tf_op jit(solution)/shard_map/ppermute | solution.py:188
  81.4 65.8 %collective-permute-start.3 = (bf16[128,768]{1,0:T(8,128)(2,1)}, bf16[128,768]{1,0:T(8,128)(2,1)}, u32[]{:S(2)}, u32[]{:S(2)}) collective-permute-start(bf16[128,768]{1,0:T(8,128)(2,1)} %slice.118), channel_id=1, source_target_pairs={{0,1},{1,2},{2,3},{3,0},{4,5},{5,6},{6,7},{7,4},{8,9},{9,10},{10,1... | collective-permute-start | bytes 589832 | tf_op jit(solution)/shard_map/ppermute | solution.py:186
  82.1 74.4 %collective-permute-start.5 = (bf16[128,768]{1,0:T(8,128)(2,1)}, bf16[128,768]{1,0:T(8,128)(2,1)}, u32[]{:S(2)}, u32[]{:S(2)}) collective-permute-start(bf16[128,768]{1,0:T(8,128)(2,1)} %slice.118), channel_id=1, source_target_pairs={{0,3},{1,0},{2,1},{3,2},{4,7},{5,4},{6,5},{7,6},{8,11},{9,8},{10,9... | collective-permute-start | bytes 589832 | tf_op jit(solution)/shard_map/ppermute | solution.py:188
  141.3 8.8 collective-permute-start.1
  147.2 9.3 collective-permute-start.4
  261.1 4.1 copy-start.1
  261.1 9.7 %slice-start = ((s8[4718592]{0:T(1024)(128)(4,1)}), s8[4194304]{0:T(1024)(128)(4,1)S(1)}, s32[]{:S(2)}) async-start(s8[4718592]{0:T(1024)(128)(4,1)} %bitcast.193), calls=%async_computation.20 | async-start | bytes 8388608
  265.3 5.6 slice-start.1
  265.3 5.6 copy-start.8
  265.3 5.6 copy-start.54
  265.3 5.6 copy-start.57
  274.8 7.8 copy-start.21
  285.6 4.5 copy-start.60
  296.3 60.0 %reduce-scatter.29.cloned.1.call-start = ((), (), s32[]{:S(2)}) async-start(), calls=%async_computation.17 | async-start | bytes 983040
  297.5 4.5 copy-start.32
  305.6 73.4 %reduce-scatter.27.cloned.1.call-start = ((), (), s32[]{:S(2)}) async-start(), calls=%async_computation.16 | async-start | bytes 983040
  336.4 71.7 %reduce-scatter.25.cloned.1.call-start = ((), (), s32[]{:S(2)}) async-start(), calls=%async_computation.15 | async-start | bytes 983040
  337.5 4.6 copy-start.30
  345.7 168.1 %reduce-scatter.19.cloned.1.call-start = ((), (), s32[]{:S(2)}) async-start(), calls=%async_computation.12 | async-start | bytes 2433024 | tf_op jit(solution)/shard_map/reduce_scatter | solution.py:352
  349.3 289.2 %reduce-scatter.33.cloned.1.call-start = ((), (), s32[]{:S(2)}) async-start(), calls=%async_computation.19 | async-start | bytes 7299072
  424.3 355.7 %reduce-scatter.21.cloned.1.call-start = ((), (), s32[]{:S(2)}) async-start(), calls=%async_computation.13 | async-start | bytes 9732096 | tf_op jit(solution)/shard_map/reduce_scatter | solution.py:352
  432.5 489.0 %reduce-scatter.23.cloned.1.call-start = ((), (), s32[]{:S(2)}) async-start(), calls=%async_computation.14 | async-start | bytes 9732096 | tf_op jit(solution)/shard_map/reduce_scatter | solution.py:352
  (51 other events, 112.4 us)
Sparse Core Ops, SparseCore 0:
  10.9 62.6 all-gather.4
  76.4 54.0 all-gather.6
  133.4 63.0 all-gather.8
  199.2 61.8 all-gather.10
  296.5 25.6 reduce-scatter.30
  324.9 24.9 reduce-scatter.28
  352.8 26.1 reduce-scatter.26
  381.9 26.1 reduce-scatter.24
  413.9 99.7 reduce-scatter.18
  519.9 118.5 reduce-scatter.32
  644.9 135.0 reduce-scatter.20
  786.3 135.1 reduce-scatter.22
